TPU v7x, 256 devices: a 8x8x2 block of a 8x8x16 slice. The times are simulated.
256 devices in a mesh: groups: 2 (over z), tensor: 64 (over x, y), seq: 2 (over core).
Axes of the slice: x: 8, y: 8, z: 2, core: 2. Of those that a mesh axis runs over, the one named last changes fastest.
The devices are a block of a 8x8x16 slice.
Arguments:
- heads_out: bfloat16 [1024, 4096], P(('groups', 'seq'), 'tensor'), parts along dimension 0, may hold values from -6 to 6
- stream_in: bfloat16 [1024, 8192], P(('groups', 'seq', 'tensor')), parts along dimension 0, may hold values from -40 to 40, as said below
- proj_levels: bfloat16 [4096, 8192], P('tensor'), may hold values from -8 to 7, as said below
- proj_scale: float32 [8192], replicated, may hold values from 0.001703125 to 0.006796875
- norm_gain: float32 [8192], replicated, may hold values from 0.25 to 1.75
- gate_levels: bfloat16 [8192, 14336], P(None, 'tensor'), may hold values from -8 to 7, as said below
- gate_scale: float32 [14336], P('tensor'), may hold values from 0.0012153398 to 0.004861359
- gate_index: int32 [64, 8], P('tensor'), may hold values from 0 to 223, as said below
- gate_extra: bfloat16 [8192, 512], P(None, 'tensor'), may hold values from -0.29882812 to 0.29882812
- up_levels: bfloat16 [8192, 14336], P(None, 'tensor'), may hold values from -8 to 7, as said below
- up_scale: float32 [14336], P('tensor'), may hold values from 0.0012153398 to 0.004861359
- up_index: int32 [64, 8], P('tensor'), may hold values from 0 to 223, as said below
- up_extra: bfloat16 [8192, 512], P(None, 'tensor'), may hold values from -0.29882812 to 0.29882812
- down_levels: bfloat16 [14336, 8192], P('tensor'), may hold values from -8 to 7, as said below
- down_scale: float32 [8192], replicated, may hold values from 0.0009020067 to 0.003591323
- down_index: int32 [64, 8], P('tensor'), may hold values from 0 to 8191, as said below
- down_extra: bfloat16 [14336, 8], P('tensor'), may hold values from -0.29882812 to 0.29882812
Outputs:
- stream_out: bfloat16 [1024, 8192], P(('groups', 'seq', 'tensor')), parts along dimension 0
There are 2 independent parts, one for each index of `groups`. A program takes and returns all parts, laid end to end along the dimension named above; an argument that names none is the same for every part. Nothing has to cross between parts.
Inputs may be any that keep to these rules, and one draw needn't show every extreme that they name: stream_in has rows and columns of differing scales. `proj_levels`: integer values. `gate_levels`: integer values. `up_levels`: integer values. `down_levels`: integer values. `gate_index`: each row holds 8 different numbers. `up_index`: each row holds 8 different numbers. `down_index`: each row holds 8 different numbers.
All inputs are finite; a program needn't handle non-finite values.
Results may differ from a plain program's by a relative error of at most 0.0055.
Values may be sent and summed in bfloat16 or wider, within the bound.
A program may use at most 128 MiB of HBM per device.

v0:
```python
import jax
import jax.numpy as jnp
from jax import lax
from jax.sharding import Mesh
from jax.sharding import PartitionSpec as P

TENSOR = ("tensor_0", "tensor_1")
GROUPS_SEQ_TENSOR = ("groups", "seq", "tensor_0", "tensor_1")


def own_rows_2(running, axes):
    for axis in axes:
        running = lax.psum_scatter(running, axis, scatter_dimension=0, tiled=True)
    return running


def rms_norm(mixed, norm_gain):
    mean_sq = jnp.mean(mixed * mixed, axis=-1, keepdims=True)
    return (mixed * lax.rsqrt(mean_sq + 1e-05) * norm_gain).astype(jnp.bfloat16)


def picker(index_row, width):
    return (index_row[:, None] == jnp.arange(width, dtype=jnp.int32)[None, :]).astype(jnp.float32)


def project(rows_in, levels, scale, extra, chosen):
    base = jnp.dot(rows_in, levels, preferred_element_type=jnp.float32)
    added = jnp.dot(rows_in, extra, preferred_element_type=jnp.float32)
    return base * scale + jnp.dot(added, chosen, precision=lax.Precision.HIGHEST)


def local(
    heads_out,
    stream_in,
    proj_levels,
    proj_scale,
    norm_gain,
    gate_levels,
    gate_scale,
    gate_index,
    gate_extra,
    up_levels,
    up_scale,
    up_index,
    up_extra,
    down_levels,
    down_scale,
    down_index,
    down_extra,
):
    shard_width = gate_levels.shape[1]
    model_width = proj_levels.shape[1]
    gate_pick = picker(gate_index[0], shard_width)
    up_pick = picker(up_index[0], shard_width)
    down_pick = picker(down_index[0], model_width)
    taken = heads_out
    proj = own_rows_2(
        jnp.dot(taken, proj_levels, preferred_element_type=jnp.float32) * proj_scale, TENSOR
    )
    mixed = stream_in.astype(jnp.float32) + proj
    normed = rms_norm(mixed, norm_gain)
    normed_rows = lax.all_gather(normed, TENSOR, axis=0, tiled=True)
    gate = project(normed_rows, gate_levels, gate_scale, gate_extra, gate_pick)
    up = project(normed_rows, up_levels, up_scale, up_extra, up_pick)
    hidden = (jax.nn.silu(gate) * up).astype(jnp.bfloat16)
    taken = hidden
    down = own_rows_2(project(taken, down_levels, down_scale, down_extra, down_pick), TENSOR)
    return (mixed + down).astype(jnp.bfloat16)


def solution(mesh):
    torus = Mesh(
        mesh.devices.reshape(mesh.shape["groups"], 8, 8, mesh.shape["seq"]),
        ("groups", "tensor_0", "tensor_1", "seq"),
    )
    return jax.shard_map(
        local,
        mesh=torus,
        in_specs=(
            P(("groups", "seq"), TENSOR),
            P(GROUPS_SEQ_TENSOR, None),
            P(TENSOR, None),
            P(),
            P(),
            P(None, TENSOR),
            P(TENSOR),
            P(TENSOR, None),
            P(None, TENSOR),
            P(None, TENSOR),
            P(TENSOR),
            P(TENSOR, None),
            P(None, TENSOR),
            P(TENSOR, None),
            P(),
            P(TENSOR, None),
            P(TENSOR, None),
        ),
        out_specs=P(GROUPS_SEQ_TENSOR, None),
        check_vma=False,
    )
```

profile of v0, /device:TPU:514, one launch (start us, length us, event | category | flops | bytes accessed | tf_op | source)
XLA Modules:
  0.0 497.5 jit_solution(14102043110908546794)
XLA Ops:
  6.6 1.2 copy-done
  7.8 5.3 %convolution_multiply_fusion.1 = f32[256,8192]{1,0:T(8,128)} fusion(bf16[256,64]{0,1:T(8,128)(2,1)} %param.17, bf16[64,8192]{1,0:T(8,128)(2,1)S(1)} %copy-done, f32[8192]{0:T(1024)} %param.20), kind=kOutput, calls=%fused_computation.2 | convolution fusion | flops 270532608 | bytes 9502720 | tf_op jit(solution)/shard_map/dot_general | solution.py:58
  13.2 112.5 %reduce-scatter.3.cloned.1.call-done = f32[32,8192]{1,0:T(8,128)} async-done(((f32[256,8192]{1,0:T(8,128)}), f32[32,8192]{1,0:T(8,128)}) %reduce-scatter.3.cloned.1.call-update) | async-done | bytes 1048592 | tf_op jit(solution)/shard_map/reduce_scatter | solution.py:13
  125.8 0.6 dynamic-slice
  127.0 80.4 %all-reduce.5.cloned.1.call-done = f32[32,8192]{1,0:T(8,128)} async-done(((f32[32,8192]{1,0:T(8,128)}), f32[32,8192]{1,0:T(8,128)}) %all-reduce.5.cloned.1.call-update) | async-done | bytes 1048592
  207.4 1.1 multiply_reduce_fusion
  208.6 1.7 fusion.4
  210.3 0.1 reduce-scatter.5.cloned.1.call-start
  210.4 81.7 %all-gather.3.cloned.1.call-done = bf16[64,4,8192]{2,1,0:T(4,128)(2,1)} async-done(((bf16[1,4,8192]{2,1,0:T(4,128)(2,1)}), bf16[64,4,8192]{2,1,0:T(4,128)(2,1)}) %all-gather.3.cloned.1.call-update) | async-done | bytes 4194320 | tf_op jit(solution)/shard_map/all_gather | solution.py:62
  292.1 7.0 %reshape.17 = bf16[256,8192]{1,0:T(8,128)(2,1)} reshape(bf16[64,4,8192]{2,1,0:T(4,128)(2,1)} %all-gather.3.cloned.1.call-done) | data formatting | bytes 8388608
  299.1 3.6 fusion.8
  302.7 1.2 fusion.7
  303.9 1.6 convolution_multiply_fusion.2
  305.5 0.4 copy-done.10
  306.0 1.4 convolution_multiply_fusion.3
  307.4 0.4 convolution_add_fusion.2
  307.8 0.4 fusion.1
  308.1 0.2 fusion.9
  308.4 1.3 convolution_multiply_fusion
  309.7 5.9 %convolution_add_fusion = f32[256,8192]{1,0:T(8,128)} fusion(f32[256,8192]{1,0:T(8,128)S(1)} %convolution_multiply_fusion, f32[256,8]{1,0:T(8,128)S(1)} %fusion.9, s32[8]{0:T(128)S(1)} %bitcast.23), kind=kOutput, calls=%fused_computation | convolution fusion | flops 203489280 | bytes 16785440 | tf_op jit(solution)/shard_map/dot_general | solution.py:29
  315.6 0.1 all-reduce.7.cloned.1.call-start
  315.7 91.8 %reduce-scatter.5.cloned.1.call-done = f32[32,8192]{1,0:T(8,128)} async-done(((f32[256,8192]{1,0:T(8,128)}), f32[32,8192]{1,0:T(8,128)}) %reduce-scatter.5.cloned.1.call-update) | async-done | bytes 1048592 | tf_op jit(solution)/shard_map/reduce_scatter | solution.py:13
  407.6 81.7 %all-reduce.7.cloned.1.call-done = f32[32,8192]{1,0:T(8,128)} async-done(((f32[32,8192]{1,0:T(8,128)}), f32[32,8192]{1,0:T(8,128)}) %all-reduce.7.cloned.1.call-update) | async-done | bytes 1048592
  489.2 1.7 fusion.2
  (41 shorter events, 0.5 us)
Async XLA Ops:
  6.5 1.2 copy-start
  6.6 119.1 %reduce-scatter.3.cloned.1.call-start = ((), (), s32[]{:S(2)}) async-start(), calls=%async_computation.2 | async-start | bytes 9437184 | tf_op jit(solution)/shard_map/reduce_scatter | solution.py:13
  13.1 112.7 %copy-start.16 = (u32[256]{0:T(256)S(1)}, u32[256]{0:T(256)}, u32[]{:S(2)}) copy-start(u32[256]{0:T(256)} %constant.24) | copy-start | bytes 3076
  13.1 194.4 %copy-start.3 = (bf16[4,8192]{1,0:T(4,128)(2,1)S(1)}, bf16[4,8192]{1,0:T(4,128)(2,1)}, u32[]{:S(2)}) copy-start(bf16[4,8192]{1,0:T(4,128)(2,1)} %param.18) | copy-start | bytes 196612
  13.1 195.5 %copy-start.5 = (f32[8192]{0:T(1024)S(1)}, f32[8192]{0:T(1024)}, u32[]{:S(2)}) copy-start(f32[8192]{0:T(1024)} %param.21) | copy-start | bytes 98308
  13.1 194.3 %all-reduce.5.cloned.1.call-start = ((), (), s32[]{:S(2)}) async-start(), calls=%async_computation.5 | async-start | bytes 2097152
  125.7 166.3 %all-gather.3.cloned.1.call-start = ((), (), s32[]{:S(2)}) async-start(), calls=%async_computation.4 | async-start | bytes 4259840 | tf_op jit(solution)/shard_map/all_gather | solution.py:62
  210.3 88.7 %copy-start.11 = (bf16[8192,8]{0,1:T(8,128)(2,1)S(1)}, bf16[8192,8]{0,1:T(8,128)(2,1)}, u32[]{:S(2)}) copy-start(bf16[8192,8]{0,1:T(8,128)(2,1)} %param.29) | copy-start | bytes 393220
  210.3 197.2 %reduce-scatter.5.cloned.1.call-start = ((), (), s32[]{:S(2)}) async-start(), calls=%async_computation.3 | async-start | bytes 9437184 | tf_op jit(solution)/shard_map/reduce_scatter | solution.py:13
  292.1 10.6 %copy-start.12 = (bf16[8192,8]{0,1:T(8,128)(2,1)S(1)}, bf16[8192,8]{0,1:T(8,128)(2,1)}, u32[]{:S(2)}) copy-start(bf16[8192,8]{0,1:T(8,128)(2,1)} %param.25) | copy-start | bytes 393220
  299.1 3.6 copy-start.1
  299.1 4.8 copy-start.9
  299.1 4.8 copy-start.13
  303.9 2.0 copy-start.10
  303.9 2.0 copy-start.14
  305.9 1.4 copy-start.8
  305.9 1.8 copy-start.15
  305.9 2.2 copy-start.6
  305.9 2.4 copy-start.2
  306.0 2.4 copy-start.4
  308.4 1.3 copy-start.7
  315.6 173.6 %all-reduce.7.cloned.1.call-start = ((), (), s32[]{:S(2)}) async-start(), calls=%async_computation.6 | async-start | bytes 2097152
Sparse Core Ops, SparseCore 0:
  13.2 112.3 reduce-scatter.2
  128.0 79.3 all-reduce.4
  210.4 81.5 all-gather.2
  315.7 91.7 reduce-scatter.4
  409.7 79.4 all-reduce.6
where the time goes:
time: 498 us
  waiting for transfers between devices  448 us (90%)
  matrix products  21.1 us (4%)
  between operations  14 us (3%)
  local copies, waits for them, and re-layouts  9.28 us (2%)
    reduce_scatter x2, waiting for transfers between devices, own_rows_2(): running = lax.psum_scatter(running, axis, scatter_dimension=0, tiled=True)  204 us
    unnamed x7, waiting for transfers between devices  162 us
    all_gather x1, waiting for transfers between devices, local(): normed_rows = lax.all_gather(normed, TENSOR, axis=0, tiled=True)  81.7 us
  transfers between devices with their start and end apart: 5, of which 5 were waited for; matrix products, arithmetic and copies ran while one was open for 0% of the time, Pallas kernels for 0%

commit v1 on v0

--- a/solution.py
+++ b/solution.py
@@ -59,7 +59,15 @@
     )
     mixed = stream_in.astype(jnp.float32) + proj
     normed = rms_norm(mixed, norm_gain)
-    normed_rows = lax.all_gather(normed, TENSOR, axis=0, tiled=True)
+    normed_rows = jnp.concatenate(
+        lax.all_to_all(
+            jnp.stack([normed] * lax.axis_size(TENSOR), axis=0),
+            axis_name=TENSOR,
+            split_axis=0,
+            concat_axis=0,
+        ),
+        0,
+    )
     gate = project(normed_rows, gate_levels, gate_scale, gate_extra, gate_pick)
     up = project(normed_rows, up_levels, up_scale, up_extra, up_pick)
     hidden = (jax.nn.silu(gate) * up).astype(jnp.bfloat16)

time: 498 us -> 524 us (1.052)
  blocking collectives: 0 us -> 103 us
  waiting for transfers between devices: 448 us -> 370 us
    all_to_all x0 -> x1, blocking collectives: none -> 103 us  [local(): lax.all_to_all(jnp.stack([normed] * lax.axis_size(TENSOR), axis=0), axis_...]
    all_gather x1 -> x0, waiting for transfers between devices: 81.7 us -> none  [local(): normed_rows = lax.all_gather(normed, TENSOR, axis=0, tiled=True)]
    unnamed x36 -> x35, local copies, waits for them, and re-layouts: 9.28 us -> 2.28 us
    reshape x0 -> x1, local copies, waits for them, and re-layouts: none -> 6.99 us  [local(): jnp.concatenate(lax.all_to_all(jnp.stack([normed] * lax.axis_size(TENSOR)...]
    unnamed x7 -> x6, waiting for transfers between devices: 162 us -> 162 us
  transfers between devices with their start and end apart: 5 -> 4, of which waited for: 5 -> 4; matrix products, arithmetic and copies ran while one was open for 0% -> 0% of each run, Pallas kernels for 0% -> 0%
where the time goes in v1:
time: 524 us; the launch traced here: 523 us
  waiting for transfers between devices  370 us (71%)
  blocking collectives  103 us (20%)
  matrix products  21.1 us (4%)
  between operations  14 us (3%)
  local copies, waits for them, and re-layouts  11.3 us (2%)
    reduce_scatter x2, waiting for transfers between devices, own_rows_2(): running = lax.psum_scatter(running, axis, scatter_dimension=0, tiled=True)  208 us
    unnamed x6, waiting for transfers between devices  162 us
    all_to_all x1, blocking collectives, local(): lax.all_to_all(jnp.stack([normed] * lax.axis_size(TENSOR), axis=0), axis_...  103 us
  transfers between devices with their start and end apart: 4, of which 4 were waited for; matrix products, arithmetic and copies ran while one was open for 0% of the time, Pallas kernels for 0%

profile of v1, /device:TPU:514, one launch (start us, length us, event | category | flops | bytes accessed | tf_op | source)
XLA Modules:
  0.0 523.1 jit_solution(14027163551749863295)
XLA Ops:
  6.6 1.2 copy-done
  7.8 5.3 %convolution_multiply_fusion.1 = f32[256,8192]{1,0:T(8,128)} fusion(bf16[256,64]{0,1:T(8,128)(2,1)} %param.17, bf16[64,8192]{1,0:T(8,128)(2,1)S(1)} %copy-done, f32[8192]{0:T(1024)} %param.20), kind=kOutput, calls=%fused_computation.2 | convolution fusion | flops 270532608 | bytes 9502720 | tf_op jit(solution)/shard_map/dot_general | solution.py:58
  13.2 112.5 %reduce-scatter.3.cloned.1.call-done = f32[32,8192]{1,0:T(8,128)} async-done(((f32[256,8192]{1,0:T(8,128)}), f32[32,8192]{1,0:T(8,128)}) %reduce-scatter.3.cloned.1.call-update) | async-done | bytes 1048592 | tf_op jit(solution)/shard_map/reduce_scatter | solution.py:13
  125.8 0.6 dynamic-slice
  127.0 80.5 %all-reduce.5.cloned.1.call-done = f32[32,8192]{1,0:T(8,128)} async-done(((f32[32,8192]{1,0:T(8,128)}), f32[32,8192]{1,0:T(8,128)}) %all-reduce.5.cloned.1.call-update) | async-done | bytes 1048592
  207.5 1.1 multiply_reduce_fusion
  208.6 1.1 multiply_convert_fusion
  209.7 2.0 stack.2
  211.7 102.8 %all_to_all.5 = bf16[64,4,8192]{2,1,0:T(4,128)(2,1)} all-to-all(bf16[64,4,8192]{2,1,0:T(4,128)(2,1)S(1)} %stack.2), channel_id=1, replica_groups=mesh['groups'=2,'tensor_0'=8,'tensor_1'=8,'seq'=2] {'tensor_0','tensor_1'}, dimensions={0} | all-to-all | bytes 8388608 | tf_op jit(solution)/shard_map/all_to_all | solution.py:63
  314.6 7.0 %reshape.21 = bf16[256,8192]{1,0:T(8,128)(2,1)} reshape(bf16[64,4,8192]{2,1,0:T(4,128)(2,1)} %all_to_all.5) | data formatting | bytes 8388608 | tf_op jit(solution)/shard_map/reshape | solution.py:62
  321.6 3.6 fusion.7
  325.1 1.2 fusion.6
  326.4 1.6 convolution_multiply_fusion.2
  328.0 0.4 copy-done.10
  328.5 1.4 convolution_multiply_fusion.3
  329.9 0.4 convolution_add_fusion.2
  330.3 0.4 fusion.1
  330.6 0.2 fusion.8
  330.9 1.3 convolution_multiply_fusion
  332.2 5.9 %convolution_add_fusion = f32[256,8192]{1,0:T(8,128)} fusion(f32[256,8192]{1,0:T(8,128)S(1)} %convolution_multiply_fusion, f32[256,8]{1,0:T(8,128)S(1)} %fusion.8, s32[8]{0:T(128)S(1)} %bitcast.21), kind=kOutput, calls=%fused_computation | convolution fusion | flops 203489280 | bytes 16785440 | tf_op jit(solution)/shard_map/dot_general | solution.py:29
  338.1 0.1 all-reduce.7.cloned.1.call-start
  338.2 95.0 %reduce-scatter.5.cloned.1.call-done = f32[32,8192]{1,0:T(8,128)} async-done(((f32[256,8192]{1,0:T(8,128)}), f32[32,8192]{1,0:T(8,128)}) %reduce-scatter.5.cloned.1.call-update) | async-done | bytes 1048592 | tf_op jit(solution)/shard_map/reduce_scatter | solution.py:13
  433.3 81.6 %all-reduce.7.cloned.1.call-done = f32[32,8192]{1,0:T(8,128)} async-done(((f32[32,8192]{1,0:T(8,128)}), f32[32,8192]{1,0:T(8,128)}) %all-reduce.7.cloned.1.call-update) | async-done | bytes 1048592
  514.9 1.7 fusion.2
  (40 shorter events, 0.4 us)
Async XLA Ops:
  6.5 1.2 copy-start
  6.6 119.1 %reduce-scatter.3.cloned.1.call-start = ((), (), s32[]{:S(2)}) async-start(), calls=%async_computation.3 | async-start | bytes 9437184 | tf_op jit(solution)/shard_map/reduce_scatter | solution.py:13
  13.0 112.7 %copy-start.16 = (u32[256]{0:T(256)S(1)}, u32[256]{0:T(256)}, u32[]{:S(2)}) copy-start(u32[256]{0:T(256)} %constant.24) | copy-start | bytes 3076
  13.0 194.4 %copy-start.3 = (bf16[4,8192]{1,0:T(4,128)(2,1)S(1)}, bf16[4,8192]{1,0:T(4,128)(2,1)}, u32[]{:S(2)}) copy-start(bf16[4,8192]{1,0:T(4,128)(2,1)} %param.18) | copy-start | bytes 196612
  13.0 195.6 %copy-start.5 = (f32[8192]{0:T(1024)S(1)}, f32[8192]{0:T(1024)}, u32[]{:S(2)}) copy-start(f32[8192]{0:T(1024)} %param.21) | copy-start | bytes 98308
  13.1 194.4 %all-reduce.5.cloned.1.call-start = ((), (), s32[]{:S(2)}) async-start(), calls=%async_computation.5 | async-start | bytes 2097152
  125.7 307.5 %reduce-scatter.5.cloned.1.call-start = ((), (), s32[]{:S(2)}) async-start(), calls=%async_computation.4 | async-start | bytes 9437184 | tf_op jit(solution)/shard_map/reduce_scatter | solution.py:13
  314.6 7.0 %copy-start.11 = (bf16[8192,8]{0,1:T(8,128)(2,1)S(1)}, bf16[8192,8]{0,1:T(8,128)(2,1)}, u32[]{:S(2)}) copy-start(bf16[8192,8]{0,1:T(8,128)(2,1)} %param.29) | copy-start | bytes 393220
  314.6 10.6 %copy-start.12 = (bf16[8192,8]{0,1:T(8,128)(2,1)S(1)}, bf16[8192,8]{0,1:T(8,128)(2,1)}, u32[]{:S(2)}) copy-start(bf16[8192,8]{0,1:T(8,128)(2,1)} %param.25) | copy-start | bytes 393220
  321.5 3.6 copy-start.1
  321.5 4.8 copy-start.9
  321.6 4.8 copy-start.13
  326.4 2.0 copy-start.10
  326.4 2.0 copy-start.14
  328.4 1.4 copy-start.8
  328.4 1.8 copy-start.15
  328.4 2.2 copy-start.6
  328.4 2.4 copy-start.2
  328.4 2.4 copy-start.4
  330.9 1.3 copy-start.7
  338.1 176.8 %all-reduce.7.cloned.1.call-start = ((), (), s32[]{:S(2)}) async-start(), calls=%async_computation.6 | async-start | bytes 2097152
Sparse Core Ops, SparseCore 0:
  13.2 112.3 reduce-scatter.2
  128.0 79.4 all-reduce.4
  338.2 94.9 reduce-scatter.4
  435.5 79.3 all-reduce.6
